TPU v7x, 32 devices: a whole 2x2x4 slice. The times are simulated.
32 devices in a mesh: expert: 8 (over z, x), replica: 4 (over y, core).
Axes of the slice: x: 2, y: 2, z: 4, core: 2. Of those that a mesh axis runs over, the one named last changes fastest.
Arguments:
- mantissa: bfloat16 [1048576, 128], P(('expert', 'replica')), may hold values from -4 to 4
- scales: bfloat16 [1048576], P(('expert', 'replica')), may hold values from 0.25 to 4
- counts: int32 [2048], P(('expert', 'replica')), may hold values from 256 to 512, as said below
- owner_map: int32 [1024], replicated, may hold values from 0 to 1023, each once
Outputs:
- out_mantissa: bfloat16 [32768, 128], P(('expert', 'replica'))
- out_scales: float32 [32768], P(('expert', 'replica'))
Inputs may be any that keep to these rules, and one draw needn't show every extreme that they name: A device's live blocks of an expert are that expert's first counts blocks; some expert has 512 live blocks on every device, and some expert has its last block dead on every device. `owner_map`: each of 0 to 1023 appears once.
All inputs are finite; a program needn't handle non-finite values. Where the computation divides by a largest or mean magnitude, that divisor is 1e-20 or more.
Results may differ from a plain program's by a relative error of at most 0.001.
Values may be sent and summed in bfloat16 or wider, within the bound.
A program may use at most 128 MiB of HBM per device.

v0:
```python
import jax
import jax.numpy as jnp
from jax import lax
from jax.sharding import PartitionSpec as P

GROUP = 32


clip_target = 0.05
epsilon = 1e-06


def by_groups(array, group_ids):
    shape = array.shape
    grouped = array.reshape((shape[0] // GROUP, GROUP) + shape[1:])
    picked = jnp.take(grouped, group_ids, axis=0)
    return picked.reshape((group_ids.shape[0] * GROUP,) + shape[1:])


def local(mantissa, scales, counts, owner_map):
    block_total = mantissa.shape[0]
    expert_count = counts.shape[0]
    per_expert = block_total // expert_count
    block_width = mantissa.shape[1]
    n_expert = lax.axis_size("expert")
    n_replica = lax.axis_size("replica")
    sources = n_expert * n_replica
    owned_rows = block_total // sources
    count_table = lax.all_gather(counts, ("expert", "replica"), axis=0, tiled=True).reshape(
        sources, expert_count
    )
    position = jnp.arange(per_expert, dtype=jnp.int32)
    is_live = (counts[:, None] > position[None, :]).reshape(block_total)
    live_scale = jnp.where(is_live, scales, jnp.zeros_like(scales))
    values = by_groups(mantissa, owner_map).astype(jnp.float32)
    summed = lax.psum_scatter(
        values * by_groups(live_scale, owner_map).astype(jnp.float32)[:, None],
        ("expert", "replica"),
        scatter_dimension=0,
        tiled=True,
    )
    my_groups = lax.dynamic_slice_in_dim(
        owner_map,
        lax.axis_index(("expert", "replica")) * (owned_rows // GROUP),
        owned_rows // GROUP,
    )
    my_blocks = (my_groups[:, None] * GROUP + jnp.arange(GROUP, dtype=jnp.int32)[None, :]).reshape(
        owned_rows
    )
    expert_loads = jnp.take(count_table, my_blocks // per_expert, axis=1)
    contributors = jnp.sum(
        (expert_loads > (my_blocks % per_expert)[None, :]).astype(jnp.int32), axis=0
    )
    averaged = summed / jnp.maximum(contributors, 1).astype(jnp.float32)[:, None]
    square_total = lax.psum(jnp.sum(averaged * averaged), ("expert", "replica"))
    root_mean = jnp.sqrt(square_total / (block_total * block_width) + epsilon)
    clip_factor = jnp.minimum(1.0, clip_target / root_mean)
    clipped = averaged * clip_factor
    block_peak = jnp.max(jnp.abs(clipped), axis=1) + epsilon
    return ((clipped / block_peak[:, None]).astype(jnp.bfloat16), block_peak)


def solution(mesh):
    in_specs = (
        P(("expert", "replica"), None),
        P(("expert", "replica")),
        P(("expert", "replica")),
        P(),
    )
    out_specs = (P(("expert", "replica"), None), P(("expert", "replica")))
    return jax.shard_map(local, mesh=mesh, in_specs=in_specs, out_specs=out_specs, check_vma=False)
```

profile of v0, /device:TPU:0, one launch (start us, length us, event | category | flops | bytes accessed | tf_op | source)
XLA Modules:
  0.0 281.8 jit_solution(12469156312380794800)
XLA Ops:
  7.2 0.0 reduce-scatter.2.cloned.1.call-start
  7.2 0.7 fusion.2
  7.9 0.7 compare_and_fusion.1
  8.6 0.2 broadcast_in_dim.45
  8.8 0.2 broadcast_in_dim.46
  9.0 0.7 fusion
  9.8 0.9 broadcast_select_fusion
  10.7 0.2 reshape.153
  10.8 13.3 %gather_fusion = bf16[1024,32,128]{2,1,0:T(8,128)(2,1)} fusion(bf16[1024,32,128]{2,1,0:T(8,128)(2,1)} %bitcast.9, s32[1024]{0:T(1024)S(1)} %fusion.2), kind=kCustom, calls=%fused_computation | custom fusion | bytes 16781312 | tf_op jit(solution)/shard_map/jit(_take)/gather | solution.py:16
  24.1 3.2 %gather_fusion.1 = bf16[1024,32]{1,0:T(8,128)(2,1)S(1)} fusion(bf16[1024,32]{1,0:T(8,128)(2,1)S(1)} %reshape.153, s32[1024]{0:T(1024)S(1)} %fusion.2), kind=kCustom, calls=%fused_computation.1 | custom fusion | bytes 135168 | tf_op jit(solution)/shard_map/jit(_take)/gather | solution.py:16
  27.3 0.2 gather.19
  27.5 13.2 %convert_multiply_fusion = f32[32768,128]{1,0:T(8,128)} fusion(bf16[1024,32,128]{2,1,0:T(8,128)(2,1)} %gather_fusion, f32[32768]{0:T(1024)S(1)} %select_convert_fusion, pred[32768]{0:T(1024)(128)(4,1)S(1)} %broadcast_in_dim.46), kind=kLoop, calls=%fused_computation.3 | loop fusion | flops 12582912 | bytes 25329664 | tf_op jit(solution)/shard_map/mul | solution.py:37
  40.6 0.0 copy-start.1
  40.6 0.0 reduce-scatter.2.cloned.1.call-update
  40.7 0.8 dynamic-slice_multiply_fusion
  41.4 0.1 iota_add_fusion
  41.5 0.1 add.119
  41.6 0.1 add.116
  41.7 0.0 copy-done.1
  41.7 0.2 dynamic-update-slice
  41.9 50.6 %all-reduce = s32[2048]{0:T(1024)S(1)} all-reduce(s32[2048]{0:T(1024)S(1)} %dynamic-update-slice), channel_id=1, replica_groups=mesh['expert'=8,'replica'=4] {'expert','replica'}, use_global_device_ids=true, to_apply=%add | all-reduce | flops 2048 | bytes 16384
  92.5 0.1 reshape.154
  92.6 0.1 copy.6
  92.8 2.8 gather_fusion.2
  95.6 0.5 convert_reduce_fusion
  96.1 132.6 %reduce-scatter.2.cloned.1.call-done = f32[1024,128]{1,0:T(8,128)} async-done(((f32[32768,128]{1,0:T(8,128)}), f32[1024,128]{1,0:T(8,128)}) %reduce-scatter.2.cloned.1.call-update) | async-done | bytes 524304 | tf_op jit(solution)/shard_map/reduce_scatter | solution.py:36
  228.7 1.9 multiply_reduce_fusion
  230.6 40.2 %psum.7 = f32[]{:T(128)} all-reduce(f32[]{:T(128)} %multiply_reduce_fusion), channel_id=1, replica_groups=mesh['expert'=8,'replica'=4] {'expert','replica'}, use_global_device_ids=true, to_apply=%region_3.4 | all-reduce | flops 1 | bytes 8 | tf_op jit(solution)/shard_map/psum | solution.py:55
  271.4 1.4 abs_reduce_fusion
  272.8 0.0 copy-start
  272.9 2.1 divide_convert_fusion
  274.9 0.0 copy-done
  (9 shorter events, 0.1 us)
Async XLA Ops:
  7.2 221.5 %reduce-scatter.2.cloned.1.call-start = ((), (), s32[]{:S(2)}) async-start(), calls=%async_computation.1 | async-start | bytes 17301504 | tf_op jit(solution)/shard_map/reduce_scatter | solution.py:36
  40.6 1.0 copy-start.1
  272.8 2.1 copy-start
Sparse Core Ops, SparseCore 0:
  40.8 187.8 reduce-scatter.1
where the time goes:
time: 282 us
  waiting for transfers between devices  133 us (47%)
  blocking collectives  90.8 us (32%)
  other arithmetic  22.9 us (8%)
  local copies, waits for them, and re-layouts  20.6 us (7%)
  between operations  14.9 us (5%)
    reduce_scatter x1, waiting for transfers between devices, local(): lax.psum_scatter(values * by_groups(live_scale, owner_map).astype(jnp.flo...  133 us
    unnamed x1, blocking collectives  50.6 us
    psum x1, blocking collectives, local(): square_total = lax.psum(jnp.sum(averaged * averaged), ('expert', 'replica'))  40.2 us
    gather x3, local copies, waits for them, and re-layouts, by_groups(): picked = jnp.take(grouped, group_ids, axis=0)  16.6 us
    mul x1, other arithmetic, local(): values * by_groups(live_scale, owner_map).astype(jnp.float32)[:, None]  13.2 us
  transfers between devices with their start and end apart: 1, of which 1 were waited for; matrix products, arithmetic and copies ran while one was open for 2% of the time, Pallas kernels for 0%

commit v1 on v0

v1 whole, which is shorter than its diff:
```python
import functools

import jax
import jax.numpy as jnp
from jax import lax
from jax.experimental import pallas as pl
from jax.experimental.pallas import tpu as pltpu
from jax.sharding import PartitionSpec as P

GROUP = 32
LANES = 128
MESH = pl.DeviceIdType.MESH
clip_target = 0.05
epsilon = 1e-06
LOADS = 4

STREAMS = (("zxy", 2), ("xyz", 4), ("yxz", 4), ("zyx", 2), ("xyz", 3), ("yxz", 3))


def split_rows(rows):
    total = sum(share for _, share in STREAMS)
    cuts, seen = [0], 0
    for _, share in STREAMS:
        seen += share
        cuts.append((rows * seen // total) // 8 * 8)
    cuts[-1] = rows
    return cuts


def kernel(sizes, cuts, owned, live_rows, total_entries, map_ref, mant_ref, table_ref, out_ref, peak_ref,
           own, other, own_table, other_table, acc, part, parts, *rest):
    extents = dict(zip("zxy", sizes))
    n_stream = len(STREAMS)
    recv1, recv2, recv3 = rest[:n_stream], rest[n_stream:2 * n_stream], rest[2 * n_stream:3 * n_stream]
    sems = rest[3 * n_stream:6 * n_stream]
    load_sem, peer_send, peer_recv, table_sem, part_send, part_recv = rest[6 * n_stream:]
    expert, replica = lax.axis_index("expert"), lax.axis_index("replica")
    X, Y = extents["x"], extents["y"]
    n_replica = 2 * Y
    n_device = extents["z"] * X * n_replica
    me = expert * n_replica + replica
    core = replica % 2
    at = {"z": expert // X, "x": expert % X, "y": replica // 2}

    def device(pos, c):
        return (pos["z"] * X + pos["x"], pos["y"] * 2 + c)

    groups = mant_ref.shape[0]
    piece = groups // LOADS
    loads = [
        pltpu.make_async_copy(mant_ref.at[pl.ds(i * piece, piece)], own.at[pl.ds(i * piece, piece)], load_sem.at[i])
        for i in range(LOADS)
    ]
    loads.append(pltpu.make_async_copy(table_ref.at[core], own_table, load_sem.at[LOADS]))

    barrier = pltpu.get_barrier_semaphore()

    def greet(i, _):
        d = (me + i) % n_device
        pl.semaphore_signal(barrier, inc=1, device_id=(d // n_replica, d % n_replica), device_id_type=MESH)
        return 0

    lax.fori_loop(1, n_device, greet, 0)
    for c in loads:
        c.start()
    pl.semaphore_wait(barrier, n_device - 1)
    peer = device(at, 1 - core)
    swaps = [
        pltpu.make_async_remote_copy(
            src_ref=mant_ref.at[pl.ds(i * piece, piece)], dst_ref=other.at[pl.ds(i * piece, piece)],
            send_sem=peer_send.at[i], recv_sem=peer_recv.at[i], device_id=peer, device_id_type=MESH)
        for i in range(LOADS)
    ]
    swaps.append(pltpu.make_async_remote_copy(
        src_ref=table_ref.at[1 - core], dst_ref=other_table,
        send_sem=peer_send.at[LOADS], recv_sem=peer_recv.at[LOADS], device_id=peer, device_id_type=MESH))
    for c in swaps:
        c.start()
    for c in loads:
        c.wait()
    for c in swaps:
        c.wait()

    per_chunk = owned // GROUP

    def build(k, _):
        z, x, y = k // (X * Y), (k // Y) % X, k % Y
        base = (k * 2 + core) * per_chunk
        mine, theirs = own_table[k, :GROUP, :], other_table[k, :GROUP, :]
        for i in range(per_chunk):
            g = map_ref[base + i]
            value = own[g].astype(jnp.float32) * mine[:, i:i + 1]
            value += other[g].astype(jnp.float32) * theirs[:, i:i + 1]
            acc[z, x, y, i * GROUP:(i + 1) * GROUP, :] = value
        acc[z, x, y, owned:, :] = own_table[k, GROUP:, :] + other_table[k, GROUP:, :]
        return 0

    lax.fori_loop(0, sizes[0] * X * Y, build, 0)

    first, steps, finish = [], [], []

    def block(where, lo, rows, whole):
        idx = []
        for axis in "zxy":
            idx.append(slice(None) if axis in whole else where[axis])
        return acc.at[tuple(idx) + (pl.ds(lo, rows),)]

    def make_stream(s, order, lo, rows):
        a, b, c = order
        na, nb, nc = (extents[t] for t in order)

        def copy(level, up, axis, d, j=None):
            n = extents[axis]
            pos = dict(at)
            pos[axis] = jnp.clip(at[axis] + (1 if up else -1), 0, n - 1)
            where = dict(at)
            where[axis] = d
            if level == 0:
                where[b] = j
            whole = (c,) if level < 2 else ()
            slot = (0 if up else n - 1) + (d - 1 if up else d)
            dst = (recv1, recv2, recv3)[level][s]
            sem = sems[3 * s + level]
            index = (slot, j) if level == 0 else (slot,)
            return pltpu.make_async_remote_copy(
                src_ref=block(where, lo, rows, whole), dst_ref=dst.at[index],
                send_sem=sem.at[(0,) + index], recv_sem=sem.at[(1,) + index],
                device_id=device(pos, core), device_id_type=MESH), dst.at[index], block(where, lo, rows, whole)

        def send(level, up, axis, d, cond, j=None):
            @pl.when(cond)
            def _():
                copy(level, up, axis, d, j)[0].start()

            def done():
                @pl.when(cond)
                def _():
                    copy(level, up, axis, d, j)[0].wait_send()
            finish.append(done)

        def take(level, up, axis, d, cond, j=None):
            @pl.when(cond)
            def _():
                c_, got, into = copy(level, up, axis, d, j)
                c_.wait_recv()
                if level < 2:
                    for i in range(nc):
                        into[i] = into[i] + got[i]
                else:
                    into[...] = into[...] + got[...]

        def ways(axis):
            n = extents[axis]
            return [(True, d) for d in range(n - 1, 0, -1)] + [(False, d) for d in range(n - 1)]

        def edge(axis, up):
            return at[axis] == (0 if up else extents[axis] - 1)

        def initial(level, axis, j=None):
            for up, d in ways(axis):
                send(level, up, axis, d, edge(axis, up), j)

        def inner(level, axis, j=None):
            n, p = extents[axis], at[axis]
            for up, d in ways(axis):
                has = jnp.logical_and(p >= 1, d >= p) if up else jnp.logical_and(p <= n - 2, d <= p)
                take(level, up, axis, d, has, j)
                onward = jnp.logical_and(p >= 1, d > p) if up else jnp.logical_and(p <= n - 2, d < p)
                if n > 2:
                    send(level, up, axis, d, onward, j)

        t1, t2, t3 = (na - 1) * nb * nc, (nb - 1) * nc, nc - 1
        for o in range(nb - 1, -1, -1):
            j = (at[b] + o) % nb
            first.append((s, lambda j=j: initial(0, a, j)))
            steps.append((rows * t1 * (nb - o) / nb, lambda j=j: inner(0, a, j)))
        if nb == 2:
            key1 = rows * t1 * 0.5
        else:
            key1 = rows * t1
        steps.append((key1 + 0.001, lambda: initial(1, b)))
        steps.append((rows * (t1 + t2) * 1.0, lambda: (inner(1, b), initial(2, c))))
        steps.append((rows * (t1 + t2 + 2 * t3) * 1.0, lambda: inner(2, c)))

    started = {}
    for s, (order, _) in enumerate(STREAMS):
        begin = len(steps)
        make_stream(s, order, cuts[s], cuts[s + 1] - cuts[s])
        offset = started.get(order[0], 0)
        for i in range(begin, len(steps)):
            steps[i] = (steps[i][0] + offset, steps[i][1])
        na, nb, nc = (extents[t] for t in order)
        started[order[0]] = offset + (cuts[s + 1] - cuts[s]) * (na - 1) * nb * nc
    for _, run in first:
        run()
    for _, run in sorted(steps, key=lambda item: item[0]):
        run()

    mine = acc.at[at["z"], at["x"], at["y"]]
    eye = lax.broadcasted_iota(jnp.int32, (LANES, LANES), 0) == lax.broadcasted_iota(jnp.int32, (LANES, LANES), 1)
    blocks = owned // LANES
    squares = jnp.zeros((8, LANES), jnp.float32)
    for i in range(blocks):
        count = mine[owned + i:owned + i + 1, :]
        column = jnp.sum(jnp.where(eye, jnp.broadcast_to(count, (LANES, LANES)), 0.0), axis=1, keepdims=True)
        rows = pl.ds(i * LANES, LANES)
        averaged = mine[rows, :] / jnp.maximum(column, 1.0)
        mine[rows, :] = averaged
        squares += jnp.sum((averaged * averaged).reshape(LANES // 8, 8, LANES), axis=0)
    part[...] = squares

    def scalar_copy(d, sender):
        return pltpu.make_async_remote_copy(
            src_ref=part, dst_ref=parts.at[sender], send_sem=part_send.at[d], recv_sem=part_recv.at[sender],
            device_id=(d // n_replica, d % n_replica), device_id_type=MESH)

    def tell(i, _):
        scalar_copy((me + i) % n_device, me).start()
        return 0

    lax.fori_loop(1, n_device, tell, 0)
    parts[me] = squares
    for run in finish:
        run()

    def hear(i, _):
        d = (me + i) % n_device
        c = scalar_copy(d, d)
        c.wait_send()
        c.wait_recv()
        return 0

    lax.fori_loop(1, n_device, hear, 0)
    square_total = jnp.sum(jnp.sum(parts[...], axis=0), keepdims=True).reshape(1, 1)
    root_mean = jnp.sqrt(square_total / total_entries + epsilon)
    clip_factor = jnp.minimum(1.0, clip_target / root_mean)
    for i in range(blocks):
        rows = pl.ds(i * LANES, LANES)
        clipped = mine[rows, :] * clip_factor
        peak = jnp.max(jnp.abs(clipped), axis=1, keepdims=True) + epsilon
        out_ref[rows, :] = (clipped / peak).astype(jnp.bfloat16)
        peak_ref[i:i + 1, :] = jnp.sum(
            jnp.where(eye, jnp.broadcast_to(peak, (LANES, LANES)), 0.0), axis=0, keepdims=True)


def local(sizes, mantissa, scales, counts, owner_map):
    block_total, width = mantissa.shape
    experts = counts.shape[0]
    per_expert = block_total // experts
    chips = sizes[0] * sizes[1] * sizes[2]
    owned = block_total // (2 * chips)
    groups = block_total // GROUP
    per_chunk = owned // GROUP
    live_rows = -(-owned // LANES // 8) * 8
    position = jnp.arange(per_expert, dtype=jnp.int32)
    live = (counts[:, None] > position[None, :]).reshape(groups, GROUP)
    table = jnp.concatenate(
        [jnp.where(live, scales.reshape(groups, GROUP), jnp.zeros((), scales.dtype)), live.astype(scales.dtype)], axis=1)
    pick = (owner_map[:, None] == jnp.arange(groups, dtype=jnp.int32)[None, :]).astype(scales.dtype)
    placed = jnp.dot(pick, table, preferred_element_type=jnp.float32)
    by_chunk = placed.reshape(chips, 2, per_chunk, 2, GROUP)
    factor = jnp.pad(by_chunk[:, :, :, 0].transpose(1, 0, 3, 2), ((0, 0),) * 3 + ((0, LANES - per_chunk),))
    alive = by_chunk[:, :, :, 1].transpose(1, 0, 2, 3).reshape(2, chips, owned // LANES, LANES)
    alive = jnp.pad(alive, ((0, 0), (0, 0), (0, live_rows - owned // LANES), (0, 0)))
    packed = jnp.concatenate([factor, alive], axis=2)

    height = owned + live_rows
    cuts = split_rows(height)
    extents = dict(zip("zxy", sizes))
    recv1, recv2, recv3, sems = [], [], [], []
    for s, (order, _) in enumerate(STREAMS):
        rows = cuts[s + 1] - cuts[s]
        na, nb, nc = (extents[t] for t in order)
        recv1.append(pltpu.VMEM((2 * (na - 1), nb, nc, rows, width), jnp.float32))
        recv2.append(pltpu.VMEM((2 * (nb - 1), nc, rows, width), jnp.float32))
        recv3.append(pltpu.VMEM((2 * (nc - 1), rows, width), jnp.float32))
        sems.append(pltpu.SemaphoreType.DMA((2, 2 * (na - 1), nb)))
        sems.append(pltpu.SemaphoreType.DMA((2, 2 * (nb - 1))))
        sems.append(pltpu.SemaphoreType.DMA((2, 2 * (nc - 1))))
    dma = pltpu.SemaphoreType.DMA
    table_shape = packed.shape[1:]
    devices = 2 * chips
    out, peak = pl.pallas_call(
        functools.partial(kernel, sizes, cuts, owned, live_rows, float(block_total * width)),
        out_shape=(
            jax.ShapeDtypeStruct((owned, width), jnp.bfloat16),
            jax.ShapeDtypeStruct((owned // LANES, LANES), jnp.float32),
        ),
        in_specs=[
            pl.BlockSpec(memory_space=pltpu.SMEM),
            pl.BlockSpec(memory_space=pl.ANY),
            pl.BlockSpec(memory_space=pl.ANY),
        ],
        out_specs=[pl.BlockSpec(memory_space=pltpu.VMEM)] * 2,
        scratch_shapes=[
            pltpu.VMEM((groups, GROUP, width), jnp.bfloat16),
            pltpu.VMEM((groups, GROUP, width), jnp.bfloat16),
            pltpu.VMEM(table_shape, jnp.float32),
            pltpu.VMEM(table_shape, jnp.float32),
            pltpu.VMEM(tuple(sizes) + (height, width), jnp.float32),
            pltpu.VMEM((8, width), jnp.float32),
            pltpu.VMEM((devices, 8, width), jnp.float32),
            *recv1, *recv2, *recv3, *sems,
            dma((LOADS + 1,)), dma((LOADS + 1,)), dma((LOADS + 1,)), dma((1,)), dma((devices,)), dma((devices,)),
        ],
        compiler_params=pltpu.CompilerParams(
            collective_id=0, has_side_effects=True, vmem_limit_bytes=62 * 1024 * 1024),
    )(owner_map, mantissa.reshape(groups, GROUP, width), packed)
    return out, peak.reshape(owned)


def solution(mesh):
    y = mesh.shape["replica"] // 2
    x = y
    z = mesh.shape["expert"] // x
    in_specs = (
        P(("expert", "replica"), None),
        P(("expert", "replica")),
        P(("expert", "replica")),
        P(),
    )
    out_specs = (P(("expert", "replica"), None), P(("expert", "replica")))
    return jax.shard_map(functools.partial(local, (z, x, y)), mesh=mesh, in_specs=in_specs, out_specs=out_specs,
                         check_vma=False)
```

time: 282 us -> 169 us (0.60)
  Pallas kernels: 0 us -> 158 us
  waiting for transfers between devices: 133 us -> 0 us
  blocking collectives: 90.8 us -> 0 us
  other arithmetic: 22.9 us -> 1.31 us
  between operations: 14.9 us -> 0.7 us
  local copies, waits for them, and re-layouts: 20.6 us -> 6.53 us
    pallas_call x0 -> x1, Pallas kernels: none -> 158 us  [local(): pl.pallas_call(functools.partial(kernel, sizes, cuts, owned, live_rows, f...]
    reduce_scatter x1 -> x0, waiting for transfers between devices: 133 us -> none  [local(): lax.psum_scatter(values * by_groups(live_scale, owner_map).astype(jnp.flo...]
    unnamed x1 -> x0, blocking collectives: 50.6 us -> none
    psum x1 -> x0, blocking collectives: 40.2 us -> none  [local(): square_total = lax.psum(jnp.sum(averaged * averaged), ('expert', 'replica'))]
    gather x4 -> x0, local copies, waits for them, and re-layouts: 19.4 us -> none  [the longest x3 16.6 us: by_groups(): picked = jnp.take(grouped, group_ids, axis=0)]
    mul x2 -> x0, other arithmetic: 13.9 us -> none  [the longest x1 13.2 us: local(): values * by_groups(live_scale, owner_map).astype(jnp.float32)[:, None]]
    unnamed x7 -> x3, local copies, waits for them, and re-layouts: 0.29 us -> 3.25 us
  transfers between devices with their start and end apart: 1 -> 0, of which waited for: 1 -> 0; matrix products, arithmetic and copies ran while one was open for 2% -> 0% of each run, Pallas kernels for 0% -> 0%
where the time goes in v1:
time: 169 us; the launch traced here: 168 us
  Pallas kernels  158 us (93%)
  local copies, waits for them, and re-layouts  6.53 us (4%)
  matrix products  1.76 us (1%)
    pallas_call x1, Pallas kernels, local(): pl.pallas_call(functools.partial(kernel, sizes, cuts, owned, live_rows, f...  158 us

profile of v1, /device:TPU:0, one launch (start us, length us, event | category | flops | bytes accessed | tf_op | source)
XLA Modules:
  0.0 168.3 jit_solution(8408370419503088341)
XLA Ops:
  0.6 0.7 gt.26
  1.4 0.1 gt.27
  1.4 0.2 fusion.2
  1.7 1.0 reshape.26
  2.7 0.2 fusion.3
  2.9 1.8 %fusion = f32[1024,64]{0,1:T(8,128)S(1)} fusion(s32[1024]{0:T(1024)} %map_ref.1, bf16[1024,32]{1,0:T(8,128)(2,1)S(1)} %fusion.2, bf16[1024,32]{1,0:T(8,128)(2,1)S(1)} %fusion.3), kind=kOutput, calls=%fused_computation.1 | convolution fusion | flops 135528448 | bytes 397312 | tf_op jit(solution)/shard_map/dot_general | solution.py:260
  4.6 0.9 reshape.27
  5.5 0.1 slice_bitcast_fusion
  5.6 0.3 copy.8
  6.0 0.2 reshape.28
  6.1 0.3 copy.11
  6.5 0.9 select_maximum_fusion.table_ref
  7.3 158.0 %shard_map.59 = (bf16[1024,128]{1,0:T(8,128)(2,1)}, f32[8,128]{1,0:T(8,128)}) custom-call(s32[1024]{0:T(1024)} %map_ref.1, bf16[1024,32,128]{2,1,0:T(8,128)(2,1)} %bitcast.21, f32[2,16,40,128]{3,2,1,0:T(8,128)} %select_maximum_fusion.table_ref), custom_call_target="tpu_custom_call" | custom-call | tf_op jit(solution)/shard_map/pallas_call | solution.py:283
  165.4 1.7 copy.14
  167.0 1.3 copy.15
  (1 shorter events, 0.0 us)

commit v2 on v1

--- a/solution.py
+++ b/solution.py
@@ -28,7 +28,7 @@
 
 
 def kernel(sizes, cuts, owned, live_rows, total_entries, map_ref, mant_ref, table_ref, out_ref, peak_ref,
-           own, other, own_table, other_table, acc, part, parts, *rest):
+           own, picked, other, own_table, other_table, acc, part, parts, *rest):
     extents = dict(zip("zxy", sizes))
     n_stream = len(STREAMS)
     recv1, recv2, recv3 = rest[:n_stream], rest[n_stream:2 * n_stream], rest[2 * n_stream:3 * n_stream]
@@ -65,37 +65,53 @@
         c.start()
     pl.semaphore_wait(barrier, n_device - 1)
     peer = device(at, 1 - core)
-    swaps = [
-        pltpu.make_async_remote_copy(
-            src_ref=mant_ref.at[pl.ds(i * piece, piece)], dst_ref=other.at[pl.ds(i * piece, piece)],
-            send_sem=peer_send.at[i], recv_sem=peer_recv.at[i], device_id=peer, device_id_type=MESH)
-        for i in range(LOADS)
-    ]
-    swaps.append(pltpu.make_async_remote_copy(
+    table_swap = pltpu.make_async_remote_copy(
         src_ref=table_ref.at[1 - core], dst_ref=other_table,
-        send_sem=peer_send.at[LOADS], recv_sem=peer_recv.at[LOADS], device_id=peer, device_id_type=MESH))
-    for c in swaps:
-        c.start()
+        send_sem=table_sem.at[0], recv_sem=table_sem.at[1], device_id=peer, device_id_type=MESH)
+    table_swap.start()
     for c in loads:
         c.wait()
-    for c in swaps:
-        c.wait()
 
     per_chunk = owned // GROUP
-
-    def build(k, _):
-        z, x, y = k // (X * Y), (k // Y) % X, k % Y
-        base = (k * 2 + core) * per_chunk
-        mine, theirs = own_table[k, :GROUP, :], other_table[k, :GROUP, :]
-        for i in range(per_chunk):
-            g = map_ref[base + i]
-            value = own[g].astype(jnp.float32) * mine[:, i:i + 1]
-            value += other[g].astype(jnp.float32) * theirs[:, i:i + 1]
-            acc[z, x, y, i * GROUP:(i + 1) * GROUP, :] = value
-        acc[z, x, y, owned:, :] = own_table[k, GROUP:, :] + other_table[k, GROUP:, :]
-        return 0
-
-    lax.fori_loop(0, sizes[0] * X * Y, build, 0)
+    Z = extents["z"]
+    blocks_xy = [(ox, oy) for ox in range(X - 1, -1, -1) for oy in range(Y - 1, -1, -1)]
+
+    def place(ox, oy, t):
+        z, x, y = (at["z"] + t + 1) % Z, (at["x"] + ox) % X, (at["y"] + oy) % Y
+        return z, x, y, (z * X + x) * Y + y
+
+    def swap(k):
+        return pltpu.make_async_remote_copy(
+            src_ref=picked.at[k], dst_ref=other.at[k], send_sem=peer_send.at[k], recv_sem=peer_recv.at[k],
+            device_id=peer, device_id_type=MESH)
+
+    def gather(ox, oy):
+        def one(t, _):
+            k = place(ox, oy, t)[3]
+            base = (k * 2 + 1 - core) * per_chunk
+            for i in range(per_chunk):
+                picked[k, i] = own[map_ref[base + i]]
+            swap(k).start()
+            return 0
+        lax.fori_loop(0, Z, one, 0)
+
+    def build(ox, oy):
+        def one(t, _):
+            z, x, y, k = place(ox, oy, t)
+            swap(k).wait_recv()
+            base = (k * 2 + core) * per_chunk
+            mine, theirs = own_table[k, :GROUP, :], other_table[k, :GROUP, :]
+            for i in range(per_chunk):
+                value = own[map_ref[base + i]].astype(jnp.float32) * mine[:, i:i + 1]
+                value += other[k, i].astype(jnp.float32) * theirs[:, i:i + 1]
+                acc[z, x, y, i * GROUP:(i + 1) * GROUP, :] = value
+            acc[z, x, y, owned:, :] = own_table[k, GROUP:, :] + other_table[k, GROUP:, :]
+            return 0
+        lax.fori_loop(0, Z, one, 0)
+
+    for ox, oy in blocks_xy:
+        gather(ox, oy)
+    table_swap.wait()
 
     first, steps, finish = [], [], []
 
@@ -109,16 +125,19 @@
         a, b, c = order
         na, nb, nc = (extents[t] for t in order)
 
-        def copy(level, up, axis, d, j=None):
+        def copy(level, away, axis, d, j=None):
             n = extents[axis]
+            turned = (2 * at[axis]) // n
+            up = away * (1 - turned) + (1 - away) * turned
+            real = d * (1 - turned) + (n - 1 - d) * turned
             pos = dict(at)
-            pos[axis] = jnp.clip(at[axis] + (1 if up else -1), 0, n - 1)
+            pos[axis] = (at[axis] + 2 * up - 1 + n) % n
             where = dict(at)
-            where[axis] = d
+            where[axis] = real
             if level == 0:
                 where[b] = j
             whole = (c,) if level < 2 else ()
-            slot = (0 if up else n - 1) + (d - 1 if up else d)
+            slot = up * (real - 1) + (1 - up) * (n - 1 + real)
             dst = (recv1, recv2, recv3)[level][s]
             sem = sems[3 * s + level]
             index = (slot, j) if level == 0 else (slot,)
@@ -127,52 +146,61 @@
                 send_sem=sem.at[(0,) + index], recv_sem=sem.at[(1,) + index],
                 device_id=device(pos, core), device_id_type=MESH), dst.at[index], block(where, lo, rows, whole)
 
-        def send(level, up, axis, d, cond, j=None):
-            @pl.when(cond)
-            def _():
-                copy(level, up, axis, d, j)[0].start()
-
-            def done():
-                @pl.when(cond)
-                def _():
-                    copy(level, up, axis, d, j)[0].wait_send()
-            finish.append(done)
-
-        def take(level, up, axis, d, cond, j=None):
-            @pl.when(cond)
-            def _():
-                c_, got, into = copy(level, up, axis, d, j)
+        def when(cond, run):
+            if cond is True:
+                run()
+            elif cond is not False:
+                pl.when(cond)(run)
+
+        def send(level, away, axis, d, cond, j=None):
+            when(cond, lambda: copy(level, away, axis, d, j)[0].start())
+            finish.append(lambda: when(cond, lambda: copy(level, away, axis, d, j)[0].wait_send()))
+
+        def take(level, away, axis, d, cond, j=None):
+            def run():
+                c_, got, into = copy(level, away, axis, d, j)
                 c_.wait_recv()
                 if level < 2:
                     for i in range(nc):
                         into[i] = into[i] + got[i]
                 else:
                     into[...] = into[...] + got[...]
-
-        def ways(axis):
+            when(cond, run)
+
+        def near(axis):
+            n, p = extents[axis], at[axis]
+            turned = (2 * p) // n
+            return p * (1 - turned) + (n - 1 - p) * turned
+
+        def initial(level, axis, j=None):
             n = extents[axis]
-            return [(True, d) for d in range(n - 1, 0, -1)] + [(False, d) for d in range(n - 1)]
-
-        def edge(axis, up):
-            return at[axis] == (0 if up else extents[axis] - 1)
-
-        def initial(level, axis, j=None):
-            for up, d in ways(axis):
-                send(level, up, axis, d, edge(axis, up), j)
+            for d in range(n - 1, 0, -1):
+                send(level, 1, axis, d, True if n == 2 else near(axis) == 0, j)
 
         def inner(level, axis, j=None):
-            n, p = extents[axis], at[axis]
-            for up, d in ways(axis):
-                has = jnp.logical_and(p >= 1, d >= p) if up else jnp.logical_and(p <= n - 2, d <= p)
-                take(level, up, axis, d, has, j)
-                onward = jnp.logical_and(p >= 1, d > p) if up else jnp.logical_and(p <= n - 2, d < p)
-                if n > 2:
-                    send(level, up, axis, d, onward, j)
+            n = extents[axis]
+            half = n // 2
+            if n == 2:
+                take(level, 0, axis, 0, True, j)
+                return
+            p = near(axis)
+            for i in range(n - 1):
+                up_d, down_d = n - 1 - i, i
+                take(level, 1, axis, up_d, jnp.logical_and(p >= 1, p <= up_d), j)
+                if up_d > 1:
+                    send(level, 1, axis, up_d, jnp.logical_and(p >= 1, p < up_d), j)
+                if down_d < half:
+                    take(level, 0, axis, down_d, p >= down_d, j)
+                    if down_d < half - 1:
+                        send(level, 0, axis, down_d, p > down_d, j)
 
         t1, t2, t3 = (na - 1) * nb * nc, (nb - 1) * nc, nc - 1
         for o in range(nb - 1, -1, -1):
             j = (at[b] + o) % nb
-            first.append((s, lambda j=j: initial(0, a, j)))
+            spans = {a: range(1, na), b: (o,), c: range(nc)}
+            needs = [(ox, oy) for ox in spans["x"] for oy in spans["y"]]
+            ready = max(blocks_xy.index(n) for n in needs)
+            first.append((ready, lambda j=j: initial(0, a, j)))
             steps.append((rows * t1 * (nb - o) / nb, lambda j=j: inner(0, a, j)))
         if nb == 2:
             key1 = rows * t1 * 0.5
@@ -191,8 +219,11 @@
             steps[i] = (steps[i][0] + offset, steps[i][1])
         na, nb, nc = (extents[t] for t in order)
         started[order[0]] = offset + (cuts[s + 1] - cuts[s]) * (na - 1) * nb * nc
-    for _, run in first:
-        run()
+    for at_block, (ox, oy) in enumerate(blocks_xy):
+        build(ox, oy)
+        for ready, run in first:
+            if ready == at_block:
+                run()
     for _, run in sorted(steps, key=lambda item: item[0]):
         run()
 
@@ -222,6 +253,8 @@
     parts[me] = squares
     for run in finish:
         run()
+    for k in range(sizes[0] * X * Y):
+        swap(k).wait_send()
 
     def hear(i, _):
         d = (me + i) % n_device
@@ -294,14 +327,15 @@
         out_specs=[pl.BlockSpec(memory_space=pltpu.VMEM)] * 2,
         scratch_shapes=[
             pltpu.VMEM((groups, GROUP, width), jnp.bfloat16),
-            pltpu.VMEM((groups, GROUP, width), jnp.bfloat16),
+            pltpu.VMEM((chips, per_chunk, GROUP, width), jnp.bfloat16),
+            pltpu.VMEM((chips, per_chunk, GROUP, width), jnp.bfloat16),
             pltpu.VMEM(table_shape, jnp.float32),
             pltpu.VMEM(table_shape, jnp.float32),
             pltpu.VMEM(tuple(sizes) + (height, width), jnp.float32),
             pltpu.VMEM((8, width), jnp.float32),
             pltpu.VMEM((devices, 8, width), jnp.float32),
             *recv1, *recv2, *recv3, *sems,
-            dma((LOADS + 1,)), dma((LOADS + 1,)), dma((LOADS + 1,)), dma((1,)), dma((devices,)), dma((devices,)),
+            dma((LOADS + 1,)), dma((chips,)), dma((chips,)), dma((2,)), dma((devices,)), dma((devices,)),
         ],
         compiler_params=pltpu.CompilerParams(
             collective_id=0, has_side_effects=True, vmem_limit_bytes=62 * 1024 * 1024),

time: 169 us -> 131 us (0.78)
  Pallas kernels: 158 us -> 120 us
    pallas_call x1, Pallas kernels: 158 us -> 120 us  [local(): pl.pallas_call(functools.partial(kernel, sizes, cuts, owned, live_rows, f...]
where the time goes in v2:
time: 131 us
  Pallas kernels  120 us (92%)
  local copies, waits for them, and re-layouts  6.53 us (5%)
  matrix products  1.76 us (1%)
  other arithmetic  1.31 us (1%)
    pallas_call x1, Pallas kernels, local(): pl.pallas_call(functools.partial(kernel, sizes, cuts, owned, live_rows, f...  120 us
    unnamed x3, local copies, waits for them, and re-layouts  3.25 us

profile of v2, /device:TPU:0, one launch (start us, length us, event | category | flops | bytes accessed | tf_op | source)
XLA Modules:
  0.0 130.6 jit_solution(7453376886579193098)
XLA Ops:
  0.6 0.7 gt.26
  1.4 0.1 gt.27
  1.4 0.2 fusion.2
  1.7 1.0 reshape.26
  2.7 0.2 fusion.3
  2.9 1.8 %fusion = f32[1024,64]{0,1:T(8,128)S(1)} fusion(s32[1024]{0:T(1024)} %map_ref.1, bf16[1024,32]{1,0:T(8,128)(2,1)S(1)} %fusion.2, bf16[1024,32]{1,0:T(8,128)(2,1)S(1)} %fusion.3), kind=kOutput, calls=%fused_computation.1 | convolution fusion | flops 135528448 | bytes 397312 | tf_op jit(solution)/shard_map/dot_general | solution.py:293
  4.6 0.9 reshape.27
  5.5 0.1 slice_bitcast_fusion
  5.6 0.3 copy.8
  6.0 0.2 reshape.28
  6.1 0.3 copy.11
  6.5 0.9 select_maximum_fusion.table_ref
  7.3 120.3 %shard_map.59 = (bf16[1024,128]{1,0:T(8,128)(2,1)}, f32[8,128]{1,0:T(8,128)}) custom-call(s32[1024]{0:T(1024)} %map_ref.1, bf16[1024,32,128]{2,1,0:T(8,128)(2,1)} %bitcast.21, f32[2,16,40,128]{3,2,1,0:T(8,128)} %select_maximum_fusion.table_ref), custom_call_target="tpu_custom_call" | custom-call | tf_op jit(solution)/shard_map/pallas_call | solution.py:316
  127.7 1.7 %copy.14 = bf16[1024,128]{1,0:T(8,128)(2,1)} copy(bf16[1024,128]{1,0:T(8,128)(2,1)} %get-tuple-element.10) | data formatting | bytes 524288
  129.4 1.3 copy.15
  (1 shorter events, 0.0 us)

commit v3 on v2

--- a/solution.py
+++ b/solution.py
@@ -1,4 +1,5 @@
 import functools
+import heapq
 
 import jax
 import jax.numpy as jnp
@@ -25,6 +26,29 @@
         cuts.append((rows * seen // total) // 8 * 8)
     cuts[-1] = rows
     return cuts
+
+
+def plan(extents, cuts):
+    link, events, keys, ends = dict.fromkeys(extents, 0.0), [], {}, {}
+    for s, (order, _) in enumerate(STREAMS):
+        (a, b, c), rows = order, cuts[s + 1] - cuts[s]
+        for o in range(extents[b] - 1, -1, -1):
+            link[a] += rows * (extents[a] - 1) * extents[c]
+            heapq.heappush(events, (link[a], s, 0, o))
+            ends[s] = link[a]
+    while events:
+        t, s, level, o = heapq.heappop(events)
+        (a, b, c), rows = STREAMS[s][0], cuts[s + 1] - cuts[s]
+        if level == 1:
+            t = max(t, ends[s])
+        keys[s, level, o] = t
+        if level == 0 and o == (1 if extents[b] == 2 else 0):
+            link[b] = max(t, link[b]) + rows * (extents[b] - 1) * extents[c]
+            heapq.heappush(events, (link[b], s, 1, 0))
+        if level == 1:
+            link[c] = max(t, link[c]) + rows * (extents[c] - 1)
+            heapq.heappush(events, (link[c], s, 2, 0))
+    return keys
 
 
 def kernel(sizes, cuts, owned, live_rows, total_entries, map_ref, mant_ref, table_ref, out_ref, peak_ref,
@@ -194,31 +218,21 @@
                     if down_d < half - 1:
                         send(level, 0, axis, down_d, p > down_d, j)
 
-        t1, t2, t3 = (na - 1) * nb * nc, (nb - 1) * nc, nc - 1
         for o in range(nb - 1, -1, -1):
             j = (at[b] + o) % nb
             spans = {a: range(1, na), b: (o,), c: range(nc)}
             needs = [(ox, oy) for ox in spans["x"] for oy in spans["y"]]
             ready = max(blocks_xy.index(n) for n in needs)
             first.append((ready, lambda j=j: initial(0, a, j)))
-            steps.append((rows * t1 * (nb - o) / nb, lambda j=j: inner(0, a, j)))
-        if nb == 2:
-            key1 = rows * t1 * 0.5
-        else:
-            key1 = rows * t1
-        steps.append((key1 + 0.001, lambda: initial(1, b)))
-        steps.append((rows * (t1 + t2) * 1.0, lambda: (inner(1, b), initial(2, c))))
-        steps.append((rows * (t1 + t2 + 2 * t3) * 1.0, lambda: inner(2, c)))
-
-    started = {}
+            steps.append(((keys[s, 0, o], 0, len(steps)), lambda j=j: inner(0, a, j)))
+            if o == (1 if nb == 2 else 0):
+                steps.append(((keys[s, 0, o], 0, len(steps)), lambda: initial(1, b)))
+        steps.append(((keys[s, 1, 0], 1, len(steps)), lambda: (inner(1, b), initial(2, c))))
+        steps.append(((keys[s, 2, 0], 2, len(steps)), lambda: inner(2, c)))
+
+    keys = plan(extents, cuts)
     for s, (order, _) in enumerate(STREAMS):
-        begin = len(steps)
         make_stream(s, order, cuts[s], cuts[s + 1] - cuts[s])
-        offset = started.get(order[0], 0)
-        for i in range(begin, len(steps)):
-            steps[i] = (steps[i][0] + offset, steps[i][1])
-        na, nb, nc = (extents[t] for t in order)
-        started[order[0]] = offset + (cuts[s + 1] - cuts[s]) * (na - 1) * nb * nc
     for at_block, (ox, oy) in enumerate(blocks_xy):
         build(ox, oy)
         for ready, run in first:

time: 131 us -> 117 us (0.89)
  Pallas kernels: 120 us -> 107 us
    pallas_call x1, Pallas kernels: 120 us -> 107 us  [local(): pl.pallas_call(functools.partial(kernel, sizes, cuts, owned, live_rows, f...]
where the time goes in v3:
time: 117 us
  Pallas kernels  107 us (91%)
  local copies, waits for them, and re-layouts  6.53 us (6%)
  matrix products  1.76 us (2%)
  other arithmetic  1.31 us (1%)
    pallas_call x1, Pallas kernels, local(): pl.pallas_call(functools.partial(kernel, sizes, cuts, owned, live_rows, f...  107 us
    unnamed x3, local copies, waits for them, and re-layouts  3.25 us

profile of v3, /device:TPU:0, one launch (start us, length us, event | category | flops | bytes accessed | tf_op | source)
XLA Modules:
  0.0 117.1 jit_solution(11940349296095925762)
XLA Ops:
  0.6 0.7 gt.26
  1.4 0.1 gt.27
  1.4 0.2 fusion.2
  1.7 1.0 reshape.26
  2.7 0.2 fusion.3
  2.9 1.8 %fusion = f32[1024,64]{0,1:T(8,128)S(1)} fusion(s32[1024]{0:T(1024)} %map_ref.1, bf16[1024,32]{1,0:T(8,128)(2,1)S(1)} %fusion.2, bf16[1024,32]{1,0:T(8,128)(2,1)S(1)} %fusion.3), kind=kOutput, calls=%fused_computation.1 | convolution fusion | flops 135528448 | bytes 397312 | tf_op jit(solution)/shard_map/dot_general | solution.py:307
  4.6 0.9 reshape.27
  5.5 0.1 slice_bitcast_fusion
  5.6 0.3 copy.8
  6.0 0.2 reshape.28
  6.1 0.3 copy.11
  6.5 0.9 select_maximum_fusion.table_ref
  7.3 106.8 %shard_map.59 = (bf16[1024,128]{1,0:T(8,128)(2,1)}, f32[8,128]{1,0:T(8,128)}) custom-call(s32[1024]{0:T(1024)} %map_ref.1, bf16[1024,32,128]{2,1,0:T(8,128)(2,1)} %bitcast.21, f32[2,16,40,128]{3,2,1,0:T(8,128)} %select_maximum_fusion.table_ref), custom_call_target="tpu_custom_call" | custom-call | tf_op jit(solution)/shard_map/pallas_call | solution.py:330
  114.2 1.7 %copy.14 = bf16[1024,128]{1,0:T(8,128)(2,1)} copy(bf16[1024,128]{1,0:T(8,128)(2,1)} %get-tuple-element.10) | data formatting | bytes 524288
  115.8 1.3 %copy.15 = f32[1024]{0:T(1024)} copy(f32[1024]{0:T(1024)} %bitcast.23) | data formatting | bytes 8192
  (1 shorter events, 0.0 us)
